TPU v7x, 128 devices: a 2x2x16 block of a 8x8x16 slice. The times are simulated.
128 devices in a mesh: grp: 4 (over x, y), fiber: 16 (over z), tm: 2 (over core).
Axes of the slice: x: 2, y: 2, z: 16, core: 2. Of those that a mesh axis runs over, the one named last changes fastest.
The devices are a block of a 8x8x16 slice.
Arguments:
- samples: bfloat16 [64, 20480, 128], P('tm', ('grp', 'fiber')), parts along dimension 1, may hold values from -6 to 6
- counts: int32 [64], P(('grp', 'fiber')), parts along dimension 0, may hold values from 80 to 320
- reach_limit: int32 [20480], P(('grp', 'fiber')), parts along dimension 0, may hold values from 320 to 960
Outputs:
- coherence_real: bfloat16 [32, 20480, 960], P('tm', ('grp', 'fiber')), parts along dimension 1
- coherence_imag: bfloat16 [32, 20480, 960], P('tm', ('grp', 'fiber')), parts along dimension 1
There are 4 independent parts, one for each index of `grp`. A program takes and returns all parts, laid end to end along the dimension named above; each array names one. Nothing has to cross between parts.
All inputs are finite; a program needn't handle non-finite values.
Results may differ from a plain program's by a relative error of at most 0.0069.
Values may be sent and summed in bfloat16 or wider, within the bound.
A program may use at most 576 MiB of HBM per device.

v0:
```python
import math

import jax
import jax.numpy as jnp
from jax import lax
from jax.sharding import PartitionSpec as P

FREQS = 32
FIRST_BIN = 8


def in_one_piece(arrays, axis, split_dim, concat_dim, along):
    both = jnp.concatenate(arrays, axis=along)
    result, at, finished = (
        lax.all_to_all(both, axis, split_axis=split_dim, concat_axis=concat_dim, tiled=True),
        0,
        [],
    )
    for a in arrays:
        finished.append(lax.slice_in_dim(result, at, at + a.shape[along], axis=along))
        at += a.shape[along]
    return tuple(finished)


def from_behind(block, axis, distance):
    devices = range(lax.axis_size(axis))
    route = [(i - distance, i) for i in devices if i - distance in devices]
    return lax.ppermute(block, axis, route)


def make_table(length, bins, first_bin):
    steps_index = jnp.arange(length, dtype=jnp.int32)
    bin_index = jnp.arange(bins, dtype=jnp.int32) + first_bin
    products = steps_index[:, None] * bin_index[None, :] % length
    phases = 2.0 * math.pi * products.astype(jnp.float32) / length
    taper = 0.5 - 0.5 * jnp.cos(2.0 * math.pi * steps_index.astype(jnp.float32) / length)
    cosines = taper[:, None] * jnp.cos(phases)
    sines = -taper[:, None] * jnp.sin(phases)
    return jnp.concatenate([cosines, sines], axis=1).astype(jnp.bfloat16)


def diagonal_band(matrix):
    bins_here, rows, columns = matrix.shape
    flattened = matrix.reshape(bins_here, rows * columns)
    flattened = jnp.pad(flattened, ((0, 0), (0, rows)))
    return flattened.reshape(bins_here, rows, columns + 1)[:, :, 1 : columns - rows + 1]


def banded_products(left_real, left_imag, right_real, right_imag):
    bins_here = left_real.shape[0]
    bin_group = 8

    def tile_band(operands):
        lreal, limag, rreal, rimag = operands
        left_both = jnp.concatenate([lreal, limag], axis=1)
        left_turned = jnp.concatenate([limag, -lreal], axis=1)
        right_both = jnp.concatenate([rreal, rimag], axis=1)
        cross_real = jnp.einsum(
            "fwc,fwj->fcj", left_both, right_both, preferred_element_type=jnp.float32
        )
        cross_imag = jnp.einsum(
            "fwc,fwj->fcj", left_turned, right_both, preferred_element_type=jnp.float32
        )
        return (diagonal_band(cross_real), diagonal_band(cross_imag))

    stacked = tuple(
        (
            array.reshape((bins_here // bin_group, bin_group) + array.shape[1:])
            for array in (left_real, left_imag, right_real, right_imag)
        )
    )
    band_real, band_imag = lax.map(tile_band, stacked)
    shape_out = (bins_here,) + band_real.shape[2:]
    return (band_real.reshape(shape_out), band_imag.reshape(shape_out))


def body(samples, counts, reach_limit):
    windows_here = samples.shape[0]
    block_width = samples.shape[1]
    dft_table = make_table(samples.shape[2], FREQS, FIRST_BIN)
    raw_spectra = jnp.einsum("wcl,lg->gwc", samples, dft_table, preferred_element_type=jnp.float32)
    real_raw = raw_spectra[:FREQS]
    imag_raw = raw_spectra[FREQS:]
    level = jnp.mean(real_raw * real_raw + imag_raw * imag_raw, axis=0)
    scale = lax.rsqrt(level + 1e-06)
    active = (lax.iota(jnp.int32, block_width) < counts[0]).astype(jnp.float32)
    real_part = (real_raw * scale * active).astype(jnp.bfloat16)
    imag_part = (imag_raw * scale * active).astype(jnp.bfloat16)
    total_windows = windows_here * lax.axis_size("tm")
    real_part, imag_part = in_one_piece((real_part, imag_part), "tm", 0, 1, 2)
    pieces = []
    current = (real_part, imag_part)
    for distance in range(1, 4):
        current = from_behind((current[0], current[1]), "fiber", -1)
        pieces.append(current)
    right_real = jnp.concatenate([real_part] + [piece[0] for piece in pieces], axis=2)
    right_imag = jnp.concatenate([imag_part] + [piece[1] for piece in pieces], axis=2)
    band_real, band_imag = banded_products(real_part, imag_part, right_real, right_imag)
    wide_real = right_real.astype(jnp.float32)
    wide_imag = right_imag.astype(jnp.float32)
    power_sum = jnp.sum(wide_real * wide_real + wide_imag * wide_imag, axis=1)
    inverse_root = lax.rsqrt(power_sum / total_windows + 1e-06)
    bins_here = inverse_root.shape[0]
    own_scale = inverse_root[:, :block_width]
    partner = diagonal_band(
        jnp.broadcast_to(inverse_root[:, None, :], (bins_here, block_width, 4 * block_width))
    )
    offsets = jnp.arange(1, 3 * block_width + 1, dtype=jnp.int32)
    in_reach = (offsets[None, :] <= reach_limit[:, None]).astype(jnp.float32)
    factor = own_scale[:, :, None] * partner * in_reach[None, :, :] / math.sqrt(total_windows)
    return ((band_real * factor).astype(jnp.bfloat16), (band_imag * factor).astype(jnp.bfloat16))


def solution(mesh):
    placed = (P("tm", ("grp", "fiber"), None), P(("grp", "fiber")), P(("grp", "fiber")))
    return jax.shard_map(
        body,
        mesh=mesh,
        in_specs=placed,
        out_specs=(P("tm", ("grp", "fiber"), None), P("tm", ("grp", "fiber"), None)),
        check_vma=False,
    )
```

profile of v0, /device:TPU:69, one launch (start us, length us, event | category | flops | bytes accessed | tf_op | source)
XLA Modules:
  0.0 621.7 jit_solution(12710695986012387338)
XLA Ops:
  1.7 0.7 copy-done
  2.4 1.2 fusion.17
  4.1 0.5 multiply_convert_fusion.1
  5.4 14.3 %all_to_all.18 = bf16[32,32,640]{2,1,0:T(8,128)(2,1)S(1)} all-to-all(bf16[32,32,640]{2,1,0:T(8,128)(2,1)S(1)} %copy.13), channel_id=1, replica_groups=mesh['grp'=4,'fiber'=16,'tm'=2] {'tm'}, dimensions={0} | all-to-all | bytes 2621440 | tf_op jit(solution)/shard_map/all_to_all | solution.py:15
  20.4 1.3 collective-permute-start
  21.7 1.3 collective-permute-start.3
  23.0 18.0 %collective-permute-done = bf16[16,64,320]{2,1,0:T(8,128)(2,1)S(1)} collective-permute-done((bf16[16,64,320]{2,1,0:T(8,128)(2,1)S(1)}, bf16[16,64,320]{2,1,0:T(8,128)(2,1)S(1)}, u32[]{:S(2)}, u32[]{:S(2)}) %collective-permute-start) | collective-permute-done | bytes 655392 | tf_op jit(solution)/shard_map/ppermute | solution.py:28
  41.0 1.3 collective-permute-start.1
  42.3 15.5 %collective-permute-done.3 = bf16[16,64,320]{2,1,0:T(8,128)(2,1)S(1)} collective-permute-done((bf16[16,64,320]{2,1,0:T(8,128)(2,1)S(1)}, bf16[16,64,320]{2,1,0:T(8,128)(2,1)S(1)}, u32[]{:S(2)}, u32[]{:S(2)}) %collective-permute-start.3) | collective-permute-done | bytes 655392 | tf_op jit(solution)/shard_map/ppermute | solution.py:28
  57.9 1.3 collective-permute-start.4
  59.2 15.7 %collective-permute-done.1 = bf16[16,64,320]{2,1,0:T(8,128)(2,1)} collective-permute-done((bf16[16,64,320]{2,1,0:T(8,128)(2,1)S(1)}, bf16[16,64,320]{2,1,0:T(8,128)(2,1)}, u32[]{:S(2)}, u32[]{:S(2)}) %collective-permute-start.1) | collective-permute-done | bytes 655392 | tf_op jit(solution)/shard_map/ppermute | solution.py:28
  74.8 1.3 collective-permute-start.2
  76.1 15.5 %collective-permute-done.4 = bf16[16,64,320]{2,1,0:T(8,128)(2,1)} collective-permute-done((bf16[16,64,320]{2,1,0:T(8,128)(2,1)S(1)}, bf16[16,64,320]{2,1,0:T(8,128)(2,1)}, u32[]{:S(2)}, u32[]{:S(2)}) %collective-permute-start.4) | collective-permute-done | bytes 655392 | tf_op jit(solution)/shard_map/ppermute | solution.py:28
  91.7 1.3 collective-permute-start.5
  93.0 1.2 compare_convert_fusion
  94.3 14.3 %collective-permute-done.2 = bf16[16,64,320]{2,1,0:T(8,128)(2,1)} collective-permute-done((bf16[16,64,320]{2,1,0:T(8,128)(2,1)}, bf16[16,64,320]{2,1,0:T(8,128)(2,1)}, u32[]{:S(2)}, u32[]{:S(2)}) %collective-permute-start.2) | collective-permute-done | bytes 655392 | tf_op jit(solution)/shard_map/ppermute | solution.py:28
  108.5 4.5 concatenate.33
  113.0 12.4 %collective-permute-done.5 = bf16[16,64,320]{2,1,0:T(8,128)(2,1)} collective-permute-done((bf16[16,64,320]{2,1,0:T(8,128)(2,1)}, bf16[16,64,320]{2,1,0:T(8,128)(2,1)}, u32[]{:S(2)}, u32[]{:S(2)}) %collective-permute-start.5) | collective-permute-done | bytes 655392 | tf_op jit(solution)/shard_map/ppermute | solution.py:28
  125.4 5.8 concatenate.34
  131.2 3.5 add_reduce_fusion
  134.7 368.1 %while.14 = (s32[]{:T(128)}, f32[2,8,320,960]{3,2,1,0:T(8,128)}, f32[2,8,320,960]{3,2,1,0:T(8,128)}, bf16[2,8,64,320]{3,2,1,0:T(8,128)(2,1)}, bf16[2,8,64,320]{3...) while((s32[]{:T(128)}, f32[2,8,320,960]{3,2,1,0:T(8,128)}, ...), condition=%wide.region_2.3_spmd, body=%wide.region_1.2_spmd.sunk | while | flops 1690992640 | bytes 323195168 | solution.py:72
  134.9 1.5 copy-done.3
  136.4 1.4 dynamic-slice_bitcast_fusion.4
  137.8 1.4 dynamic-slice_bitcast_fusion.5
  139.2 0.8 constant_dynamic-slice_fusion.4
  140.0 1.3 copy.26
  141.4 1.0 bitcast_negate_fusion.2
  142.4 1.8 constant_dynamic-slice_fusion.5
  144.2 1.3 copy.27
  145.5 7.7 %convolution_bitcast_fusion.4 = f32[1,8,320,1280]{3,2,1,0:T(8,128)} fusion(bf16[8,64,1280]{2,1,0:T(8,128)(2,1)S(1)} %dynamic-slice_bitcast_fusion.4, bf16[8,64,1280]{2,1,0:T(8,128)(2,1)S(1)} %dynamic-slice_bitcast_fusion.5, bf16[8,64,320]{1,2,0:T(8,128)(2,1)} %bitcast_negate_fusion.2, bf16[8,64,320]{1,2,0:T(8,128)(2,1)S(1)} %bitcast.67), kind=kOutput, calls=%fused_computation.4.clone.1 | convolution fusion | flops 845414400 | bytes 16384000 | tf_op jit(solution)/shard_map/while/body/eval_jaxpr/fwc,fwj->fcj/dot_general | solution.py:61
  153.2 17.0 %copy.28 = f32[1,8,320,1280]{3,1,2,0:T(8,128)} copy(f32[1,8,320,1280]{3,2,1,0:T(8,128)} %convolution_bitcast_fusion.4) | data formatting | bytes 26214400 | tf_op jit(solution)/shard_map/while
  170.2 9.7 %pad.78 = f32[8,409920]{1,0:T(8,128)} pad(f32[8,409600]{1,0:T(8,128)} %bitcast.66, f32[]{:T(128)} %constant.64.clone.1..sunk), padding=0_0x0_320 | pad | bytes 26224644 | tf_op jit(solution)/shard_map/while/body/eval_jaxpr/jit(_pad)/pad | solution.py:45
  179.9 15.0 %reshape.132 = f32[3279360]{0:T(1024)} reshape(f32[8,409920]{1,0:T(8,128)} %pad.78) | data formatting | bytes 26234880 | tf_op jit(solution)/shard_map/while
  194.9 26.7 %reshape.133 = f32[8,320,1281]{2,1,0:T(8,128)} reshape(f32[3279360]{0:T(1024)} %reshape.132) | data formatting | bytes 26234880 | tf_op jit(solution)/shard_map/while/body/eval_jaxpr/reshape | solution.py:46
  221.7 7.7 %convolution_bitcast_fusion.5 = f32[1,8,320,1280]{3,2,1,0:T(8,128)} fusion(bf16[8,64,1280]{2,1,0:T(8,128)(2,1)S(1)} %dynamic-slice_bitcast_fusion.4, bf16[8,64,1280]{2,1,0:T(8,128)(2,1)S(1)} %dynamic-slice_bitcast_fusion.5, bf16[8,64,320]{1,2,0:T(8,128)(2,1)S(1)} %bitcast.68, bf16[8,64,320]{1,2,0:T(8,128)(2,1)} %bitcast.69), kind=kOutput, calls=%fused_computation.5.clone.1 | convolution fusion | flops 845414400 | bytes 16384000 | tf_op jit(solution)/shard_map/while/body/eval_jaxpr/fwc,fwj->fcj/dot_general | solution.py:58
  229.4 17.1 %copy.29 = f32[1,8,320,1280]{3,1,2,0:T(8,128)} copy(f32[1,8,320,1280]{3,2,1,0:T(8,128)} %convolution_bitcast_fusion.5) | data formatting | bytes 26214400 | tf_op jit(solution)/shard_map/while
  246.5 9.8 %pad.79 = f32[8,409920]{1,0:T(8,128)} pad(f32[8,409600]{1,0:T(8,128)} %bitcast.65, f32[]{:T(128)} %constant.64.clone.1..sunk), padding=0_0x0_320 | pad | bytes 26224644 | tf_op jit(solution)/shard_map/while/body/eval_jaxpr/jit(_pad)/pad | solution.py:45
  256.2 15.0 %reshape.134 = f32[3279360]{0:T(1024)} reshape(f32[8,409920]{1,0:T(8,128)} %pad.79) | data formatting | bytes 26234880 | tf_op jit(solution)/shard_map/while
  271.3 26.6 %reshape.135 = f32[8,320,1281]{2,1,0:T(8,128)} reshape(f32[3279360]{0:T(1024)} %reshape.134) | data formatting | bytes 26234880 | tf_op jit(solution)/shard_map/while/body/eval_jaxpr/reshape | solution.py:46
  297.8 18.6 %fusion.33 = (f32[2,8,320,960]{3,2,1,0:T(8,128)}, f32[2,8,320,960]{3,2,1,0:T(8,128)}) fusion(f32[2,8,320,960]{3,2,1,0:T(8,128)} %get-tuple-element.199, s32[]{:T(128)S(6)} %copy.35, f32[8,320,1281]{2,1,0:T(8,128)} %reshape.133, f32[2,8,320,960]{3,2,1,0:T(8,128)} %get-tuple-element.198, f32[8,320,1281]{2,1,0:T(8,128)} %reshape.135), kind=kLoop, calls=%fused_computation.1.clone.1 | loop fusion | bytes 41943044 | tf_op jit(solution)/shard_map/while/body/jit(dynamic_update_index_in_dim)/dynamic_update_slice | solution.py:72
  316.7 1.5 copy-done.3
  318.1 1.4 dynamic-slice_bitcast_fusion.4
  319.5 1.4 dynamic-slice_bitcast_fusion.5
  321.0 0.8 constant_dynamic-slice_fusion.4
  321.8 1.3 copy.26
  323.1 1.0 bitcast_negate_fusion.2
  324.2 1.8 constant_dynamic-slice_fusion.5
  326.0 1.3 copy.27
  327.3 7.7 %convolution_bitcast_fusion.4 = f32[1,8,320,1280]{3,2,1,0:T(8,128)} fusion(bf16[8,64,1280]{2,1,0:T(8,128)(2,1)S(1)} %dynamic-slice_bitcast_fusion.4, bf16[8,64,1280]{2,1,0:T(8,128)(2,1)S(1)} %dynamic-slice_bitcast_fusion.5, bf16[8,64,320]{1,2,0:T(8,128)(2,1)} %bitcast_negate_fusion.2, bf16[8,64,320]{1,2,0:T(8,128)(2,1)S(1)} %bitcast.67), kind=kOutput, calls=%fused_computation.4.clone.1 | convolution fusion | flops 845414400 | bytes 16384000 | tf_op jit(solution)/shard_map/while/body/eval_jaxpr/fwc,fwj->fcj/dot_general | solution.py:61
  335.0 17.0 %copy.28 = f32[1,8,320,1280]{3,1,2,0:T(8,128)} copy(f32[1,8,320,1280]{3,2,1,0:T(8,128)} %convolution_bitcast_fusion.4) | data formatting | bytes 26214400 | tf_op jit(solution)/shard_map/while
  352.0 9.7 %pad.78 = f32[8,409920]{1,0:T(8,128)} pad(f32[8,409600]{1,0:T(8,128)} %bitcast.66, f32[]{:T(128)} %constant.64.clone.1..sunk), padding=0_0x0_320 | pad | bytes 26224644 | tf_op jit(solution)/shard_map/while/body/eval_jaxpr/jit(_pad)/pad | solution.py:45
  361.6 15.0 %reshape.132 = f32[3279360]{0:T(1024)} reshape(f32[8,409920]{1,0:T(8,128)} %pad.78) | data formatting | bytes 26234880 | tf_op jit(solution)/shard_map/while
  376.7 26.8 %reshape.133 = f32[8,320,1281]{2,1,0:T(8,128)} reshape(f32[3279360]{0:T(1024)} %reshape.132) | data formatting | bytes 26234880 | tf_op jit(solution)/shard_map/while/body/eval_jaxpr/reshape | solution.py:46
  403.5 7.7 %convolution_bitcast_fusion.5 = f32[1,8,320,1280]{3,2,1,0:T(8,128)} fusion(bf16[8,64,1280]{2,1,0:T(8,128)(2,1)S(1)} %dynamic-slice_bitcast_fusion.4, bf16[8,64,1280]{2,1,0:T(8,128)(2,1)S(1)} %dynamic-slice_bitcast_fusion.5, bf16[8,64,320]{1,2,0:T(8,128)(2,1)S(1)} %bitcast.68, bf16[8,64,320]{1,2,0:T(8,128)(2,1)} %bitcast.69), kind=kOutput, calls=%fused_computation.5.clone.1 | convolution fusion | flops 845414400 | bytes 16384000 | tf_op jit(solution)/shard_map/while/body/eval_jaxpr/fwc,fwj->fcj/dot_general | solution.py:58
  411.2 17.1 %copy.29 = f32[1,8,320,1280]{3,1,2,0:T(8,128)} copy(f32[1,8,320,1280]{3,2,1,0:T(8,128)} %convolution_bitcast_fusion.5) | data formatting | bytes 26214400 | tf_op jit(solution)/shard_map/while
  428.3 9.7 %pad.79 = f32[8,409920]{1,0:T(8,128)} pad(f32[8,409600]{1,0:T(8,128)} %bitcast.65, f32[]{:T(128)} %constant.64.clone.1..sunk), padding=0_0x0_320 | pad | bytes 26224644 | tf_op jit(solution)/shard_map/while/body/eval_jaxpr/jit(_pad)/pad | solution.py:45
  438.0 15.0 %reshape.134 = f32[3279360]{0:T(1024)} reshape(f32[8,409920]{1,0:T(8,128)} %pad.79) | data formatting | bytes 26234880 | tf_op jit(solution)/shard_map/while
  453.0 26.4 %reshape.135 = f32[8,320,1281]{2,1,0:T(8,128)} reshape(f32[3279360]{0:T(1024)} %reshape.134) | data formatting | bytes 26234880 | tf_op jit(solution)/shard_map/while/body/eval_jaxpr/reshape | solution.py:46
  479.4 18.6 %fusion.33 = (f32[2,8,320,960]{3,2,1,0:T(8,128)}, f32[2,8,320,960]{3,2,1,0:T(8,128)}) fusion(f32[2,8,320,960]{3,2,1,0:T(8,128)} %get-tuple-element.199, s32[]{:T(128)S(6)} %copy.35, f32[8,320,1281]{2,1,0:T(8,128)} %reshape.133, f32[2,8,320,960]{3,2,1,0:T(8,128)} %get-tuple-element.198, f32[8,320,1281]{2,1,0:T(8,128)} %reshape.135), kind=kLoop, calls=%fused_computation.1.clone.1 | loop fusion | bytes 41943044 | tf_op jit(solution)/shard_map/while/body/jit(dynamic_update_index_in_dim)/dynamic_update_slice | solution.py:72
  502.8 10.7 %broadcast_in_dim.15 = f32[16,320,1280]{2,1,0:T(8,128)} broadcast(f32[16,1280]{1,0:T(8,128)S(1)} %add_rsqrt_fusion), dimensions={0,2} | broadcast | bytes 26296320 | tf_op jit(solution)/shard_map/broadcast_in_dim | solution.py:106
  513.5 21.0 %copy.21 = f32[2,8,320,1280]{3,1,2,0:T(8,128)S(1)} copy(f32[2,8,320,1280]{3,2,1,0:T(8,128)} %bitcast.71) | data formatting | bytes 52428800
  534.4 9.1 %pad.17 = f32[16,409920]{1,0:T(8,128)} pad(f32[16,409600]{1,0:T(8,128)S(1)} %bitcast.70, f32[]{:T(128)} %constant.64.clone.1), padding=0_0x0_320 | pad | bytes 52449284 | tf_op jit(solution)/shard_map/jit(_pad)/pad | solution.py:45
  543.5 47.5 %reshape.121 = f32[16,320,1281]{2,1,0:T(8,128)} reshape(f32[16,409920]{1,0:T(8,128)} %pad.17) | data formatting | bytes 52469760 | tf_op jit(solution)/shard_map/reshape | solution.py:46
  591.0 30.5 %fusion.12 = (bf16[16,320,960]{2,1,0:T(8,128)(2,1)}, bf16[16,320,960]{2,1,0:T(8,128)(2,1)}) fusion(f32[2,8,320,960]{3,2,1,0:T(8,128)} %get-tuple-element.93, f32[16,320,1281]{2,1,0:T(8,128)} %reshape.121, f32[320,960]{1,0:T(8,128)} %compare_convert_fusion, f32[16,320]{1,0:T(8,128)S(1)} %slice-done, f32[2,8,320,960]{3,2,1,0:T(8,128)} %get-tuple-element.92), kind=kLoop, calls=%fused_computation.24 | loop fusion | flops 34406400 | bytes 79892480 | tf_op jit(solution)/shard_map/convert_element_type | solution.py:111
  (53 shorter events, 2.4 us)
Async XLA Ops:
  0.6 1.8 copy-start
  19.7 73.3 %copy-start.13 = (s32[320]{0:T(512)S(1)}, s32[320]{0:T(512)}, u32[]{:S(2)}) copy-start(s32[320]{0:T(512)} %param.7) | copy-start | bytes 3844
  20.4 73.9 %copy-start.7 = (bf16[16,64,320]{2,1,0:T(8,128)(2,1)}, bf16[16,64,320]{2,1,0:T(8,128)(2,1)S(1)}, u32[]{:S(2)}) copy-start(bf16[16,64,320]{2,1,0:T(8,128)(2,1)S(1)} %get-tuple-element.136) | copy-start | bytes 1966084
  20.4 20.7 %collective-permute-start = (bf16[16,64,320]{2,1,0:T(8,128)(2,1)S(1)}, bf16[16,64,320]{2,1,0:T(8,128)(2,1)S(1)}, u32[]{:S(2)}, u32[]{:S(2)}) collective-permute-start(bf16[16,64,320]{2,1,0:T(8,128)(2,1)S(1)} %get-tuple-element.136), channel_id=1, source_target_pairs={{2,0},{4,2},{6,4},{8,6},{10,8},{12,10},{14,12},{16,14},{18,16},{20... | collective-permute-start | bytes 1966088 | tf_op jit(solution)/shard_map/ppermute | solution.py:28
  21.7 36.2 %collective-permute-start.3 = (bf16[16,64,320]{2,1,0:T(8,128)(2,1)S(1)}, bf16[16,64,320]{2,1,0:T(8,128)(2,1)S(1)}, u32[]{:S(2)}, u32[]{:S(2)}) collective-permute-start(bf16[16,64,320]{2,1,0:T(8,128)(2,1)S(1)} %get-tuple-element.135), channel_id=1, source_target_pairs={{2,0},{4,2},{6,4},{8,6},{10,8},{12,10},{14,12},{16,14},{18,16},{20... | collective-permute-start | bytes 1966088 | tf_op jit(solution)/shard_map/ppermute | solution.py:28
  41.0 53.2 %copy-start.10 = (bf16[16,64,320]{2,1,0:T(8,128)(2,1)}, bf16[16,64,320]{2,1,0:T(8,128)(2,1)S(1)}, u32[]{:S(2)}) copy-start(bf16[16,64,320]{2,1,0:T(8,128)(2,1)S(1)} %collective-permute-done) | copy-start | bytes 1966084
  41.0 33.8 %collective-permute-start.1 = (bf16[16,64,320]{2,1,0:T(8,128)(2,1)S(1)}, bf16[16,64,320]{2,1,0:T(8,128)(2,1)}, u32[]{:S(2)}, u32[]{:S(2)}) collective-permute-start(bf16[16,64,320]{2,1,0:T(8,128)(2,1)S(1)} %collective-permute-done), channel_id=1, source_target_pairs={{2,0},{4,2},{6,4},{8,6},{10,8},{12,10},{14,12},{16,14},{18,16},{20... | collective-permute-start | bytes 1966088 | tf_op jit(solution)/shard_map/ppermute | solution.py:28
  57.9 36.4 %copy-start.9 = (bf16[16,64,320]{2,1,0:T(8,128)(2,1)}, bf16[16,64,320]{2,1,0:T(8,128)(2,1)S(1)}, u32[]{:S(2)}) copy-start(bf16[16,64,320]{2,1,0:T(8,128)(2,1)S(1)} %collective-permute-done.3) | copy-start | bytes 1966084
  57.9 33.8 %collective-permute-start.4 = (bf16[16,64,320]{2,1,0:T(8,128)(2,1)S(1)}, bf16[16,64,320]{2,1,0:T(8,128)(2,1)}, u32[]{:S(2)}, u32[]{:S(2)}) collective-permute-start(bf16[16,64,320]{2,1,0:T(8,128)(2,1)S(1)} %collective-permute-done.3), channel_id=1, source_target_pairs={{2,0},{4,2},{6,4},{8,6},{10,8},{12,10},{14,12},{16,14},{18,16},{20... | collective-permute-start | bytes 1966088 | tf_op jit(solution)/shard_map/ppermute | solution.py:28
  74.8 33.7 %collective-permute-start.2 = (bf16[16,64,320]{2,1,0:T(8,128)(2,1)}, bf16[16,64,320]{2,1,0:T(8,128)(2,1)}, u32[]{:S(2)}, u32[]{:S(2)}) collective-permute-start(bf16[16,64,320]{2,1,0:T(8,128)(2,1)} %collective-permute-done.1), channel_id=1, source_target_pairs={{2,0},{4,2},{6,4},{8,6},{10,8},{12,10},{14,12},{16,14},{18,16},{20... | collective-permute-start | bytes 1966088 | tf_op jit(solution)/shard_map/ppermute | solution.py:28
  91.7 33.7 %collective-permute-start.5 = (bf16[16,64,320]{2,1,0:T(8,128)(2,1)}, bf16[16,64,320]{2,1,0:T(8,128)(2,1)}, u32[]{:S(2)}, u32[]{:S(2)}) collective-permute-start(bf16[16,64,320]{2,1,0:T(8,128)(2,1)} %collective-permute-done.4), channel_id=1, source_target_pairs={{2,0},{4,2},{6,4},{8,6},{10,8},{12,10},{14,12},{16,14},{18,16},{20... | collective-permute-start | bytes 1966088 | tf_op jit(solution)/shard_map/ppermute | solution.py:28
  134.7 368.1 %copy-start.12 = (f32[16,1280]{1,0:T(8,128)S(1)}, f32[16,1280]{1,0:T(8,128)}, u32[]{:S(2)}) copy-start(f32[16,1280]{1,0:T(8,128)} %add_reduce_fusion) | copy-start | bytes 245764
  134.9 1.5 copy-start.3
  134.9 4.3 copy-start.5
  134.9 4.3 copy-start.8
  141.4 1.1 copy-start.2
  297.8 18.6 %copy-start.4 = (bf16[2,8,64,1280]{3,2,1,0:T(8,128)(2,1)S(1)}, bf16[2,8,64,1280]{3,2,1,0:T(8,128)(2,1)}, u32[]{:S(2)}) copy-start(bf16[2,8,64,1280]{3,2,1,0:T(8,128)(2,1)} %copy-done.3) | copy-start | bytes 7864324 | tf_op jit(solution)/shard_map/while
  297.8 18.6 %copy-start.6 = (bf16[2,8,64,320]{3,2,1,0:T(8,128)(2,1)S(1)}, bf16[2,8,64,320]{3,2,1,0:T(8,128)(2,1)}, u32[]{:S(2)}) copy-start(bf16[2,8,64,320]{3,2,1,0:T(8,128)(2,1)} %copy-done.5) | copy-start | bytes 1966084 | tf_op jit(solution)/shard_map/while
  316.6 1.5 copy-start.3
  316.6 4.3 copy-start.5
  316.7 4.3 copy-start.8
  323.1 1.1 copy-start.2
  479.4 18.6 %copy-start.4 = (bf16[2,8,64,1280]{3,2,1,0:T(8,128)(2,1)S(1)}, bf16[2,8,64,1280]{3,2,1,0:T(8,128)(2,1)}, u32[]{:S(2)}) copy-start(bf16[2,8,64,1280]{3,2,1,0:T(8,128)(2,1)} %copy-done.3) | copy-start | bytes 7864324 | tf_op jit(solution)/shard_map/while
  479.4 18.6 %copy-start.6 = (bf16[2,8,64,320]{3,2,1,0:T(8,128)(2,1)S(1)}, bf16[2,8,64,320]{3,2,1,0:T(8,128)(2,1)}, u32[]{:S(2)}) copy-start(bf16[2,8,64,320]{3,2,1,0:T(8,128)(2,1)} %copy-done.5) | copy-start | bytes 1966084 | tf_op jit(solution)/shard_map/while
  502.8 10.7 %copy-start.11 = (f32[16,1280]{1,0:T(8,128)}, f32[16,1280]{1,0:T(8,128)S(1)}, u32[]{:S(2)}) copy-start(f32[16,1280]{1,0:T(8,128)S(1)} %add_rsqrt_fusion) | copy-start | bytes 245764
  543.5 47.5 %slice-start = ((f32[16,1280]{1,0:T(8,128)}), f32[16,320]{1,0:T(8,128)S(1)}, s32[]{:S(2)}) async-start(f32[16,1280]{1,0:T(8,128)} %copy-done.11), calls=%async_computation.1 | async-start | bytes 49152 | tf_op jit(solution)/shard_map/slice | solution.py:104
  591.0 30.5 %copy-start.1 = (bf16[32,320,128]{2,1,0:T(8,128)(2,1)S(1)}, bf16[32,320,128]{2,1,0:T(8,128)(2,1)}, u32[]{:S(2)}) copy-start(bf16[32,320,128]{2,1,0:T(8,128)(2,1)} %param.5) | copy-start | bytes 7864324
where the time goes:
time: 629 us; the launch traced here: 622 us
  local copies, waits for them, and re-layouts  430 us (68%)
  waiting for transfers between devices  91.4 us (15%)
  other arithmetic  38.9 us (6%)
  matrix products  31.9 us (5%)
  blocking collectives  14.3 us (2%)
  starting transfers between devices  7.8 us (1%)
    reshape x5, local copies, waits for them, and re-layouts, diagonal_band(): flattened.reshape(bins_here, rows, columns + 1)[:, :, 1:columns - rows + 1]  154 us
    while x32, local copies, waits for them, and re-layouts  131 us
    ppermute x6, waiting for transfers between devices, from_behind(): return lax.ppermute(block, axis, route)  91.4 us
    pad x5, local copies, waits for them, and re-layouts, diagonal_band(): flattened = jnp.pad(flattened, ((0, 0), (0, rows)))  47.9 us
    dynamic_update_slice x2, local copies, waits for them, and re-layouts, banded_products(): band_real, band_imag = lax.map(tile_band, stacked)  37.2 us
    convert_element_type x1, other arithmetic, body(): (band_imag * factor).astype(jnp.bfloat16)  30.5 us
    unnamed x17, local copies, waits for them, and re-layouts  21.7 us
    dot_general x2, matrix products, tile_band(): jnp.einsum('fwc,fwj->fcj', left_both, right_both, preferred_element_type=...  15.4 us
  transfers between devices with their start and end apart: 6, of which 6 were waited for; matrix products, arithmetic and copies ran while one was open for 1% of the time, Pallas kernels for 0%

commit v1 on v0

v1 whole, which is shorter than its diff:
```python
import functools
import math

import jax
import jax.numpy as jnp
from jax import lax
from jax.experimental import pallas as pl
from jax.experimental.pallas import tpu as pltpu
from jax.sharding import PartitionSpec as P


FREQS = 32
FIRST_BIN = 8

LANE = 128
SUB = 8
PAIR = (((1,), (1,)), ((), ()))
PLAIN = (((1,), (0,)), ((), ()))


def sum_pieces(x):
    square = x * x
    upper = square.astype(jnp.bfloat16)
    lower = (square - upper.astype(jnp.float32)).astype(jnp.bfloat16)
    return upper, lower


def band_kernel(n_blocks, first, total_windows, tile0, per, *refs):
    bins_here = refs[0].shape[0]

    def one(b, carry):
        band_bin(b, n_blocks, first, total_windows, tile0, per, *refs)
        return carry

    lax.fori_loop(0, bins_here, one, 0)


def band_bin(b, n_blocks, first, total_windows, tile0, per, *refs):
    left_ref, reach_ref = refs[:2]
    blocks = refs[2:2 + n_blocks]
    out_re, out_im, both, right, cols, rows_s = refs[-6:]
    rows = left_ref.shape[1]
    quarter = LANE // 4
    lo = tile0
    hi = min(tile0 + per + 3, 11)

    wide = left_ref[b].astype(jnp.float32)
    back = (SUB - 1) - lax.broadcasted_iota(jnp.int32, (SUB, LANE), 0)
    wide = jnp.concatenate([jnp.take_along_axis(wide[i:i + SUB], back, axis=0) for i in range(0, rows, SUB)], axis=0)
    lane = lax.broadcasted_iota(jnp.int32, wide.shape, 1)
    odd = (lane // quarter) % 2 == 1
    swapped = jnp.where(odd, -pltpu.roll(wide, quarter, 1), pltpu.roll(wide, LANE - quarter, 1))
    upper, lower = sum_pieces(wide)
    ones = jnp.ones((LANE, LANE), jnp.bfloat16)
    power = lax.dot_general(upper, ones, PLAIN, preferred_element_type=jnp.float32) + lax.dot_general(lower, ones, PLAIN, preferred_element_type=jnp.float32)
    rows_s[...] = lax.rsqrt(power / total_windows + 1e-6) / math.sqrt(total_windows)
    for g in range(0, rows, LANE):
        count = min(LANE, rows - g)
        both[2 * g:2 * g + count, :] = wide[g:g + count].astype(jnp.bfloat16)
        both[2 * g + count:2 * g + 2 * count, :] = swapped[g:g + count].astype(jnp.bfloat16)
    ones = jnp.ones((SUB, LANE), jnp.bfloat16)
    values = [block[b] for block in blocks]
    if first + n_blocks == 4:
        values.append(jnp.zeros((11 * LANE - 4 * rows, LANE), jnp.bfloat16))
    joined = jnp.concatenate(values, axis=0)
    for v in range(lo, hi):
        at = v * LANE - first * rows
        piece = joined[at:at + LANE]
        upper, lower = sum_pieces(piece.astype(jnp.float32))
        right[:, v * LANE:(v + 1) * LANE] = piece.T
        power = lax.dot_general(ones, upper, PAIR, preferred_element_type=jnp.float32) + lax.dot_general(ones, lower, PAIR, preferred_element_type=jnp.float32)
        cols[:, v * LANE:(v + 1) * LANE] = lax.rsqrt(power / total_windows + 1e-6)

    lane = lax.broadcasted_iota(jnp.int32, (SUB, LANE), 1)
    for part in range(per):
        tile = tile0 + part
        for g in range(0, rows, LANE):
            count = min(LANE, rows - g)
            start = g + tile * LANE
            m = lax.dot_general(both[2 * g:2 * g + 2 * count, :], right[:, start:start + 2 * LANE], PLAIN, preferred_element_type=jnp.float32)
            c0 = cols[:, start:start + LANE]
            c1 = cols[:, start + LANE:start + 2 * LANE]
            turn = []
            for i in range(0, count, SUB):
                row = back + i
                take = lane > row
                offset = jnp.where(take, lane, lane + LANE) - row + tile * LANE
                at = g + i
                factor = jnp.where(offset <= reach_ref[at:at + SUB, :], jnp.where(take, c0, c1) * rows_s[at:at + SUB, :], 0.0)
                for shift in (0, count):
                    a = m[shift + i:shift + i + SUB]
                    z = jnp.where(take, a[:, :LANE], a[:, LANE:]) * factor
                    y = pltpu.roll(z, (2 * LANE - SUB - i) % LANE, 1, stride=1, stride_axis=0)
                    turn.append(jnp.take_along_axis(y, back, axis=0))
            for which, out in enumerate((out_re, out_im)):
                out[b, g:g + count, part * LANE:(part + 1) * LANE] = jnp.concatenate(turn[which::2], axis=0).astype(jnp.bfloat16)


def band_call(left, reach, blocks, first, width, place, bin0, nb, step, outs, total_windows):
    rows, depth = left.shape[1:]
    n = len(blocks)
    bins = left.shape[0]
    in_specs = [pl.BlockSpec((step, rows, depth), lambda f: (bin0 // step + f, 0, 0)),
                pl.BlockSpec((rows, LANE), lambda f: (0, 0))]
    args = [left, reach]
    for arr, off in blocks:
        in_specs.append(pl.BlockSpec((step, rows, depth), functools.partial(lambda off, f: (off + f, 0, 0), off // step)))
        args.append(arr)
    alias = {}
    if outs is not None:
        for i, o in enumerate(outs):
            alias[len(args)] = i
            in_specs.append(pl.BlockSpec(memory_space=pl.ANY))
            args.append(o)
    out_shape = [jax.ShapeDtypeStruct((bins, rows, 3 * rows), jnp.bfloat16)] * 2
    out_specs = [pl.BlockSpec((step, rows, width), lambda f: (bin0 // step + f, 0, place))] * 2
    per = min(width, 8 * LANE - place * width) // LANE
    return pl.pallas_call(
        functools.partial(band_kernel, n, first, float(total_windows), place * width // LANE, per),
        grid=(nb // step,), in_specs=in_specs, out_specs=out_specs, out_shape=out_shape,
        input_output_aliases=alias,
        scratch_shapes=[pltpu.VMEM((2 * rows, depth), jnp.bfloat16), pltpu.VMEM((depth, 11 * LANE), jnp.bfloat16),
                        pltpu.VMEM((SUB, 11 * LANE), jnp.float32), pltpu.VMEM((rows, LANE), jnp.float32)],
        compiler_params=pltpu.CompilerParams(dimension_semantics=("arbitrary",)),
        cost_estimate=pl.CostEstimate(flops=nb * per * 300_000_000, bytes_accessed=nb * rows * width * 4, transcendentals=0),
    )(*args)


def make_table(length, bins, first_bin):
    steps_index = jnp.arange(length, dtype=jnp.int32)
    bin_index = jnp.arange(bins, dtype=jnp.int32) + first_bin
    products = steps_index[:, None] * bin_index[None, :] % length
    phases = 2.0 * math.pi * products.astype(jnp.float32) / length
    taper = 0.5 - 0.5 * jnp.cos(2.0 * math.pi * steps_index.astype(jnp.float32) / length)
    cosines = taper[:, None] * jnp.cos(phases)
    sines = -taper[:, None] * jnp.sin(phases)
    return jnp.concatenate([cosines, sines], axis=1).astype(jnp.bfloat16)


def own_spectra(samples, counts):
    windows, width = samples.shape[:2]
    table = make_table(samples.shape[2], FREQS, FIRST_BIN)
    raw = jnp.einsum("wcl,lg->gwc", samples, table, preferred_element_type=jnp.float32)
    real_raw, imag_raw = raw[:FREQS], raw[FREQS:]
    level = jnp.mean(real_raw * real_raw + imag_raw * imag_raw, axis=0)
    active = (lax.iota(jnp.int32, width) < counts[0]).astype(jnp.float32)
    scale = lax.rsqrt(level + 1e-06)
    parts = jnp.stack([real_raw, imag_raw], axis=1) * scale * active
    parts = parts.astype(jnp.bfloat16).reshape(FREQS, 2 * windows, width)
    return parts.transpose(0, 2, 1)


def body(samples, counts, reach_limit):
    rows = samples.shape[1]
    total_windows = samples.shape[0] * lax.axis_size("tm")
    mine = own_spectra(samples, counts)
    own = lax.all_to_all(mine, "tm", split_axis=0, concat_axis=2, tiled=True)
    devices = lax.axis_size("fiber")
    route = [(i, i - 1) for i in range(1, devices)]
    reach = jnp.broadcast_to(reach_limit.reshape(-1, SUB)[:, ::-1].reshape(-1, 1), (rows, LANE))
    spans = []
    at = 0
    for size in CHUNKS:
        spans.append((at, size))
        at += size
    held = [[(own, at) for at, size in spans]]
    for distance in range(3):
        if distance == 0:
            pieces = [own[at:at + size] for at, size in spans]
        else:
            pieces = [piece for piece, _ in held[-1]]
        moved = []
        for piece in pieces:
            moved.append((lax.ppermute(piece, "fiber", route), 0))
        held.append(moved)
    outs = None
    for first, last, width, place in ((0, 1, 256, 0), (0, 2, 256, 1), (1, 3, 512, 1)):
        for i, (at, size) in enumerate(spans):
            blocks = [held[d][i] for d in range(first, last + 1)]
            outs = band_call(own, reach, blocks, first, width, place, at, size, STEP, outs, total_windows)
    return tuple(outs)


CHUNKS = (10, 6)
STEP = 2


def solution(mesh):
    placed = (P("tm", ("grp", "fiber"), None), P(("grp", "fiber")), P(("grp", "fiber")))
    return jax.shard_map(
        body,
        mesh=mesh,
        in_specs=placed,
        out_specs=(P("tm", ("grp", "fiber"), None), P("tm", ("grp", "fiber"), None)),
        check_vma=False,
    )
```

time: 629 us -> 138 us (0.22); the launches traced: 622 us -> 137 us
  local copies, waits for them, and re-layouts: 430 us -> 15.5 us
  Pallas kernels: 0 us -> 47.8 us
  waiting for transfers between devices: 91.4 us -> 45.6 us
  other arithmetic: 38.9 us -> 2.92 us
  matrix products: 31.9 us -> 1.19 us
    reshape x5 -> x1, local copies, waits for them, and re-layouts: 154 us -> 0.08 us  [body(): reach_limit.reshape(-1, SUB)[:, ::-1].reshape(-1, 1)]
    while x32 -> x0, local copies, waits for them, and re-layouts: 131 us -> none
    pad x5 -> x0, local copies, waits for them, and re-layouts: 47.9 us -> none  [diagonal_band(): flattened = jnp.pad(flattened, ((0, 0), (0, rows)))]
    pallas_call x0 -> x6, Pallas kernels: none -> 47.8 us  [band_call(): pl.pallas_call(functools.partial(band_kernel, n, first, float(total_windo...]
    ppermute x6, waiting for transfers between devices: 91.4 us -> 45.6 us  [body(): moved.append((lax.ppermute(piece, 'fiber', route), 0))]
    dynamic_update_slice x2 -> x0, local copies, waits for them, and re-layouts: 37.2 us -> none  [banded_products(): band_real, band_imag = lax.map(tile_band, stacked)]
    convert_element_type x4 -> x1, other arithmetic: 32.2 us -> 0.01 us  [own_spectra(): active = (lax.iota(jnp.int32, width) < counts[0]).astype(jnp.float32)]
    dot_general x5 -> x1, matrix products: 31.9 us -> 1.19 us  [own_spectra(): jnp.einsum('wcl,lg->gwc', samples, table, preferred_element_type=jnp.floa...]
  transfers between devices with their start and end apart: 6 -> 6, of which waited for: 6 -> 3; matrix products, arithmetic and copies ran while one was open for 1% -> 6% of each run, Pallas kernels for 0% -> 29%
where the time goes in v1:
time: 138 us; the launch traced here: 137 us
  Pallas kernels  47.8 us (35%)
  waiting for transfers between devices  45.6 us (33%)
  local copies, waits for them, and re-layouts  15.5 us (11%)
  blocking collectives  14.5 us (11%)
  starting transfers between devices  7.92 us (6%)
  other arithmetic  2.92 us (2%)
  between operations  1.44 us (1%)
    pallas_call x6, Pallas kernels, band_call(): pl.pallas_call(functools.partial(band_kernel, n, first, float(total_windo...  47.8 us
    ppermute x6, waiting for transfers between devices, body(): moved.append((lax.ppermute(piece, 'fiber', route), 0))  45.6 us
    all_to_all x1, blocking collectives, body(): own = lax.all_to_all(mine, 'tm', split_axis=0, concat_axis=2, tiled=True)  14.5 us
    ppermute x6, starting transfers between devices, body(): moved.append((lax.ppermute(piece, 'fiber', route), 0))  7.92 us
    slice x6, local copies, waits for them, and re-layouts, body(): pieces = [own[at:at + size] for at, size in spans]  5.61 us
    all_to_all x2, local copies, waits for them, and re-layouts, body(): own = lax.all_to_all(mine, 'tm', split_axis=0, concat_axis=2, tiled=True)  5.31 us
    unnamed x10, local copies, waits for them, and re-layouts  3.56 us
  transfers between devices with their start and end apart: 6, of which 3 were waited for; matrix products, arithmetic and copies ran while one was open for 6% of the time, Pallas kernels for 29%

profile of v1, /device:TPU:69, one launch (start us, length us, event | category | flops | bytes accessed | tf_op | source)
XLA Modules:
  0.0 137.0 jit_solution(18027299497223130152)
XLA Ops:
  0.6 0.0 copy-start
  0.7 0.2 multiply_convert_fusion.1
  0.9 1.5 %copy-done = bf16[32,320,128]{2,1,0:T(8,128)(2,1)S(1)} copy-done((bf16[32,320,128]{2,1,0:T(8,128)(2,1)S(1)}, bf16[32,320,128]{2,1,0:T(8,128)(2,1)}, u32[]{:S(2)}) %copy-start) | copy-done | bytes 2621464
  2.4 1.2 fusion.6
  3.6 0.7 add_reduce_fusion
  4.9 0.2 pad_maximum_fusion
  5.2 1.8 %fusion.2 = bf16[32,320,64]{1,2,0:T(8,128)(2,1)S(1)} fusion(f32[32,64,320]{2,0,1:T(8,128)S(1)} %bitcast.23, f32[320]{0:T(512)S(1)} %fusion.12, f32[64,320]{1,0:T(8,128)S(1)} %bitcast.27), kind=kLoop, calls=%fused_computation.4 | loop fusion | flops 1966080 | bytes 4015360 | tf_op jit(solution)/shard_map/transpose | solution.py:150
  7.0 14.5 %all_to_all.18 = bf16[32,320,64]{1,2,0:T(8,128)(2,1)S(1)} all-to-all(bf16[32,320,64]{1,2,0:T(8,128)(2,1)S(1)} %fusion.2), channel_id=1, replica_groups=mesh['grp'=4,'fiber'=16,'tm'=2] {'tm'}, dimensions={0} | all-to-all | bytes 2621440 | tf_op jit(solution)/shard_map/all_to_all | solution.py:157
  21.5 0.0 copy-start.1
  21.5 1.1 copy-done.1
  22.7 0.1 slice.27
  22.8 1.1 copy.19
  23.8 2.2 %copy.20 = bf16[10,320,128]{2,1,0:T(8,128)(2,1)} copy(bf16[10,320,128]{1,2,0:T(8,128)(2,1)} %bitcast.25) | data formatting | bytes 1638400 | tf_op jit(solution)/shard_map/slice | solution.py:169
  26.1 1.3 collective-permute-start.3
  27.4 1.1 slice.26
  28.5 0.1 copy.17
  28.6 1.0 copy.18
  29.6 0.0 copy-start.3
  29.6 1.4 %collective-permute-start = (bf16[6,320,128]{2,1,0:T(8,128)(2,1)}, bf16[6,320,128]{2,1,0:T(8,128)(2,1)S(1)}, u32[]{:S(2)}, u32[]{:S(2)}) collective-permute-start(bf16[6,320,128]{2,1,0:T(8,128)(2,1)} %copy.18), channel_id=1, source_target_pairs={{2,0},{4,2},{6,4},{8,6},{10,8},{12,10},{14,12},{16,14},{18,16},{20... | collective-permute-start | bytes 1474568 | tf_op jit(solution)/shard_map/ppermute | solution.py:174
  31.0 2.8 %copy.16 = bf16[16,320,2,64]{1,3,2,0:T(8,128)(2,1)} copy(bf16[16,320,2,64]{1,3,0,2:T(8,128)(2,1)} %bitcast.22) | data formatting | bytes 2621440 | tf_op jit(solution)/shard_map/all_to_all | solution.py:157
  33.8 2.6 %copy.30.refs_0_.refs_2_ = bf16[16,320,128]{2,1,0:T(8,128)(2,1)} copy(bf16[16,320,128]{1,2,0:T(8,128)(2,1)} %bitcast.24) | data formatting | bytes 2621440 | tf_op jit(solution)/shard_map/all_to_all | solution.py:157
  36.3 0.0 copy-done.3
  36.3 0.1 reshape.40
  36.4 0.1 rev.3
  36.5 0.1 broadcast_in_dim.4
  36.6 21.5 %collective-permute-done.refs_3_.refs_2_ = bf16[6,320,128]{2,1,0:T(8,128)(2,1)S(1)} collective-permute-done((bf16[6,320,128]{2,1,0:T(8,128)(2,1)}, bf16[6,320,128]{2,1,0:T(8,128)(2,1)S(1)}, u32[]{:S(2)}, u32[]{:S(2)}) %collective-permute-start) | collective-permute-done | bytes 491552 | tf_op jit(solution)/shard_map/ppermute | solution.py:174
  58.1 0.0 copy-start.2
  58.1 1.3 collective-permute-start.1
  59.4 0.0 collective-permute-done.3.refs_3_.refs_2_
  59.5 1.3 collective-permute-start.4
  60.8 0.8 broadcast_in_dim.5.refs_1_
  61.6 8.4 %shard_map.50 = (bf16[16,320,960]{2,1,0:T(8,128)(2,1)}, bf16[16,320,960]{2,1,0:T(8,128)(2,1)}) custom-call(bf16[16,320,128]{2,1,0:T(8,128)(2,1)} %copy.30.refs_0_.refs_2_, s32[320,128]{1,0:T(8,128)} %broadcast_in_dim.5.refs_1_, bf16[16,320,128]{2,1,0:T(8,128)(2,1)} %copy.30.refs_0_.refs_2_, bf16[10,320,128]{2,1,0:T(8,128)(2,1)} %collective-permute-done.3.refs_3_.refs_2_), custom_call_target="tpu_custom_call" | custom-call | flops 6000000000 | bytes 3276800 | tf_op jit(solution)/shard_map/pallas_call | solution.py:118
  70.0 0.0 copy-done.2
  70.0 5.9 %shard_map.51 = (bf16[16,320,960]{2,1,0:T(8,128)(2,1)}, bf16[16,320,960]{2,1,0:T(8,128)(2,1)}) custom-call(bf16[16,320,128]{2,1,0:T(8,128)(2,1)} %copy.30.refs_0_.refs_2_, s32[320,128]{1,0:T(8,128)} %broadcast_in_dim.5.refs_1_, bf16[16,320,128]{2,1,0:T(8,128)(2,1)} %copy.30.refs_0_.refs_2_, ...), custom_call_target="tpu_custom_call", output_to_operand_aliasing={{0}: (4, {}), {1}: (5, {})} | custom-call | flops 3600000000 | bytes 1966080 | tf_op jit(solution)/shard_map/pallas_call | solution.py:118
  75.9 0.0 collective-permute-done.1.refs_4_.refs_3_
  75.9 1.3 collective-permute-start.2
  77.2 12.1 %collective-permute-done.4.refs_4_.refs_3_ = bf16[10,320,128]{2,1,0:T(8,128)(2,1)} collective-permute-done((bf16[10,320,128]{2,1,0:T(8,128)(2,1)}, bf16[10,320,128]{2,1,0:T(8,128)(2,1)}, u32[]{:S(2)}, u32[]{:S(2)}) %collective-permute-start.4) | collective-permute-done | bytes 819232 | tf_op jit(solution)/shard_map/ppermute | solution.py:174
  89.3 1.3 collective-permute-start.5
  90.6 8.7 %shard_map.52 = (bf16[16,320,960]{2,1,0:T(8,128)(2,1)}, bf16[16,320,960]{2,1,0:T(8,128)(2,1)}) custom-call(bf16[16,320,128]{2,1,0:T(8,128)(2,1)} %copy.30.refs_0_.refs_2_, s32[320,128]{1,0:T(8,128)} %broadcast_in_dim.5.refs_1_, bf16[16,320,128]{2,1,0:T(8,128)(2,1)} %copy.30.refs_0_.refs_2_, ...), custom_call_target="tpu_custom_call", output_to_operand_aliasing={{0}: (5, {}), {1}: (6, {})} | custom-call | flops 6000000000 | bytes 3276800 | tf_op jit(solution)/shard_map/pallas_call | solution.py:118
  99.2 6.0 %shard_map.53 = (bf16[16,320,960]{2,1,0:T(8,128)(2,1)}, bf16[16,320,960]{2,1,0:T(8,128)(2,1)}) custom-call(bf16[16,320,128]{2,1,0:T(8,128)(2,1)} %copy.30.refs_0_.refs_2_, s32[320,128]{1,0:T(8,128)} %broadcast_in_dim.5.refs_1_, bf16[16,320,128]{2,1,0:T(8,128)(2,1)} %copy.30.refs_0_.refs_2_, ...), custom_call_target="tpu_custom_call", output_to_operand_aliasing={{0}: (5, {}), {1}: (6, {})} | custom-call | flops 3600000000 | bytes 1966080 | tf_op jit(solution)/shard_map/pallas_call | solution.py:118
  105.3 12.0 %collective-permute-done.5.refs_4_ = bf16[10,320,128]{2,1,0:T(8,128)(2,1)S(1)} collective-permute-done((bf16[10,320,128]{2,1,0:T(8,128)(2,1)}, bf16[10,320,128]{2,1,0:T(8,128)(2,1)S(1)}, u32[]{:S(2)}, u32[]{:S(2)}) %collective-permute-start.5) | collective-permute-done | bytes 819232 | tf_op jit(solution)/shard_map/ppermute | solution.py:174
  117.3 0.0 copy-start.4
  117.3 0.9 copy-done.4
  118.1 11.2 %shard_map.54 = (bf16[16,320,960]{2,1,0:T(8,128)(2,1)}, bf16[16,320,960]{2,1,0:T(8,128)(2,1)}) custom-call(bf16[16,320,128]{2,1,0:T(8,128)(2,1)} %copy.30.refs_0_.refs_2_, s32[320,128]{1,0:T(8,128)} %broadcast_in_dim.5.refs_1_, bf16[10,320,128]{2,1,0:T(8,128)(2,1)} %collective-permute-done.3.refs_3_.refs_2_, ...), custom_call_target="tpu_custom_call", output_to_operand_aliasing={{0}: (5, {}), {1}: (6, {})} | custom-call | flops 12000000000 | bytes 6553600 | tf_op jit(solution)/shard_map/pallas_call | solution.py:118
  129.3 0.0 collective-permute-done.2.refs_4_
  129.3 7.6 %shard_map.55 = (bf16[16,320,960]{2,1,0:T(8,128)(2,1)}, bf16[16,320,960]{2,1,0:T(8,128)(2,1)}) custom-call(bf16[16,320,128]{2,1,0:T(8,128)(2,1)} %copy.30.refs_0_.refs_2_, s32[320,128]{1,0:T(8,128)} %broadcast_in_dim.5.refs_1_, bf16[6,320,128]{2,1,0:T(8,128)(2,1)} %copy-done.2, ...), custom_call_target="tpu_custom_call", output_to_operand_aliasing={{0}: (5, {}), {1}: (6, {})} | custom-call | flops 7200000000 | bytes 3932160 | tf_op jit(solution)/shard_map/pallas_call | solution.py:118
  (5 shorter events, 0.1 us)
Async XLA Ops:
  0.6 1.7 %copy-start = (bf16[32,320,128]{2,1,0:T(8,128)(2,1)S(1)}, bf16[32,320,128]{2,1,0:T(8,128)(2,1)}, u32[]{:S(2)}) copy-start(bf16[32,320,128]{2,1,0:T(8,128)(2,1)} %param.3) | copy-start | bytes 7864324
  21.5 1.1 copy-start.1
  26.1 33.4 %collective-permute-start.3 = (bf16[10,320,128]{2,1,0:T(8,128)(2,1)}, bf16[10,320,128]{2,1,0:T(8,128)(2,1)}, u32[]{:S(2)}, u32[]{:S(2)}) collective-permute-start(bf16[10,320,128]{2,1,0:T(8,128)(2,1)} %copy.20), channel_id=1, source_target_pairs={{2,0},{4,2},{6,4},{8,6},{10,8},{12,10},{14,12},{16,14},{18,16},{20... | collective-permute-start | bytes 2457608 | tf_op jit(solution)/shard_map/ppermute | solution.py:174
  29.6 6.7 %copy-start.3 = (s32[320]{0:T(512)S(1)}, s32[320]{0:T(512)}, u32[]{:S(2)}) copy-start(s32[320]{0:T(512)} %param.5) | copy-start | bytes 3844
  29.6 28.5 %collective-permute-start = (bf16[6,320,128]{2,1,0:T(8,128)(2,1)}, bf16[6,320,128]{2,1,0:T(8,128)(2,1)S(1)}, u32[]{:S(2)}, u32[]{:S(2)}) collective-permute-start(bf16[6,320,128]{2,1,0:T(8,128)(2,1)} %copy.18), channel_id=1, source_target_pairs={{2,0},{4,2},{6,4},{8,6},{10,8},{12,10},{14,12},{16,14},{18,16},{20... | collective-permute-start | bytes 1474568 | tf_op jit(solution)/shard_map/ppermute | solution.py:174
  58.1 11.9 %copy-start.2 = (bf16[6,320,128]{2,1,0:T(8,128)(2,1)}, bf16[6,320,128]{2,1,0:T(8,128)(2,1)S(1)}, u32[]{:S(2)}) copy-start(bf16[6,320,128]{2,1,0:T(8,128)(2,1)S(1)} %collective-permute-done.refs_3_.refs_2_) | copy-start | bytes 1474564
  58.1 17.7 %collective-permute-start.1 = (bf16[6,320,128]{2,1,0:T(8,128)(2,1)S(1)}, bf16[6,320,128]{2,1,0:T(8,128)(2,1)}, u32[]{:S(2)}, u32[]{:S(2)}) collective-permute-start(bf16[6,320,128]{2,1,0:T(8,128)(2,1)S(1)} %collective-permute-done.refs_3_.refs_2_), channel_id=1, source_target_pairs={{2,0},{4,2},{6,4},{8,6},{10,8},{12,10},{14,12},{16,14},{18,16},{20... | collective-permute-start | bytes 1474568 | tf_op jit(solution)/shard_map/ppermute | solution.py:174
  59.5 29.8 %collective-permute-start.4 = (bf16[10,320,128]{2,1,0:T(8,128)(2,1)}, bf16[10,320,128]{2,1,0:T(8,128)(2,1)}, u32[]{:S(2)}, u32[]{:S(2)}) collective-permute-start(bf16[10,320,128]{2,1,0:T(8,128)(2,1)} %collective-permute-done.3.refs_3_.refs_2_), channel_id=1, source_target_pairs={{2,0},{4,2},{6,4},{8,6},{10,8},{12,10},{14,12},{16,14},{18,16},{20... | collective-permute-start | bytes 2457608 | tf_op jit(solution)/shard_map/ppermute | solution.py:174
  75.9 53.5 %collective-permute-start.2 = (bf16[6,320,128]{2,1,0:T(8,128)(2,1)}, bf16[6,320,128]{2,1,0:T(8,128)(2,1)}, u32[]{:S(2)}, u32[]{:S(2)}) collective-permute-start(bf16[6,320,128]{2,1,0:T(8,128)(2,1)} %collective-permute-done.1.refs_4_.refs_3_), channel_id=1, source_target_pairs={{2,0},{4,2},{6,4},{8,6},{10,8},{12,10},{14,12},{16,14},{18,16},{20... | collective-permute-start | bytes 1474568 | tf_op jit(solution)/shard_map/ppermute | solution.py:174
  89.3 28.0 %collective-permute-start.5 = (bf16[10,320,128]{2,1,0:T(8,128)(2,1)}, bf16[10,320,128]{2,1,0:T(8,128)(2,1)S(1)}, u32[]{:S(2)}, u32[]{:S(2)}) collective-permute-start(bf16[10,320,128]{2,1,0:T(8,128)(2,1)} %collective-permute-done.4.refs_4_.refs_3_), channel_id=1, source_target_pairs={{2,0},{4,2},{6,4},{8,6},{10,8},{12,10},{14,12},{16,14},{18,16},{20... | collective-permute-start | bytes 2457608 | tf_op jit(solution)/shard_map/ppermute | solution.py:174
  117.3 0.9 copy-start.4
